TPU v7x, 32 devices: a whole 2x2x4 slice. The times are simulated.
32 devices in a mesh: ep: 4 (over x, core), fsdp: 8 (over z, y).
Axes of the slice: x: 2, y: 2, z: 4, core: 2. Of those that a mesh axis runs over, the one named last changes fastest.
Arguments:
- master_gate: float32 [128, 2048, 768], P('ep', 'fsdp'), may hold values from -0.1875 to 0.1875
- master_up: float32 [128, 2048, 768], P('ep', 'fsdp'), may hold values from -0.1875 to 0.1875
- router_weight: float32 [2048, 128], P('fsdp', 'ep'), may hold values from -0.125 to 0.125
- router_gain: float32 [2048], P('fsdp'), may hold values from 0.25 to 1.75
Outputs:
- final_gate: bfloat16 [128, 2048, 768], P(('ep', 'fsdp'))
- final_up: bfloat16 [128, 2048, 768], P(('ep', 'fsdp'))
- scale_gate: float32 [128, 768], P(('ep', 'fsdp'))
- scale_up: float32 [128, 768], P(('ep', 'fsdp'))
- serve_router: bfloat16 [2048, 128], replicated
All inputs are finite; a program needn't handle non-finite values.
Results may differ from a plain program's by a relative error of at most 0.001.
Values may be sent and summed in bfloat16 or wider, within the bound.
A program may use at most 192 MiB of HBM per device.

v0:
```python
import functools

import jax
import jax.numpy as jnp
from jax import lax
from jax.experimental import pallas as pl
from jax.experimental.pallas import tpu as pltpu
from jax.sharding import PartitionSpec as P

MESH = pl.DeviceIdType.MESH
RING = 2
SLOTS = 3


def kernel(
    groups, members, local, rows,
    gate, up, part_router,
    final_gate, final_up, scale_gate, scale_up, router,
    held, narrow, partial, arrived, scales,
    load_sem, send_sem, recv_sem,
    sum_send, sum_recv, scale_send, scale_recv,
    row_send, row_recv, col_send, col_recv, router_sem,
):
    group, me = lax.axis_index("ep"), lax.axis_index("fsdp")
    steps = 2 * local

    def peer(j):
        return lax.rem(me + j, members)

    def group_peer(j):
        return lax.rem(group + j, groups)

    def source(step):
        return (gate, up)[step // local], (final_gate, final_up)[step // local], step % local

    order = [*range(1, steps), *range(1, steps)]

    def load(step, slot, j):
        master, _, index = source(step)
        return pltpu.make_async_copy(
            master.at[peer(j) * local + index], held.at[slot, j], load_sem.at[slot, j]
        )

    def start_load(step, slot):
        @pl.loop(0, members)
        def _(j):
            load(step, slot, j).start()

    def start_place(place):
        if place < len(order):
            start_load(order[place], 1 + place % RING)

    def sum_copy(step, j):
        return pltpu.make_async_remote_copy(
            src_ref=partial.at[step, j], dst_ref=arrived.at[step, j],
            send_sem=sum_send.at[step, j], recv_sem=sum_recv.at[step, j],
            device_id=(group, peer(j)), device_id_type=MESH,
        )

    def scale_copy(step, j):
        return pltpu.make_async_remote_copy(
            src_ref=scales.at[step, 0], dst_ref=scales.at[step, j],
            send_sem=scale_send.at[step, j], recv_sem=scale_recv.at[step, j],
            device_id=(group, peer(j)), device_id_type=MESH,
        )

    def my_rows(final, index):
        return final.at[index, pl.ds(pl.multiple_of(me * rows, rows), rows), :]

    def data_copy(step, j):
        _, final, index = source(step)
        return pltpu.make_async_remote_copy(
            src_ref=narrow.at[step % SLOTS, j], dst_ref=my_rows(final, index),
            send_sem=send_sem.at[step, j], recv_sem=recv_sem.at[step, j],
            device_id=(group, peer(j)), device_id_type=MESH,
        )

    width, depth = part_router.shape
    my_group_rows = pl.ds(pl.multiple_of(group * width, width), width)
    my_block = router.at[my_group_rows, pl.ds(pl.multiple_of(me * depth, depth), depth)]

    def row_copy(j):
        return pltpu.make_async_remote_copy(
            src_ref=part_router, dst_ref=my_block, send_sem=row_send.at[j], recv_sem=row_recv.at[j],
            device_id=(group, near_peer(j)), device_id_type=MESH,
        )

    half = members // 2
    near = [*range(1, half), half]

    def near_peer(j):
        if j == half:
            return peer(half)
        return me // half * half + lax.rem(me % half + j, half)

    def relay_copy(j):
        other = pl.ds(pl.multiple_of(peer(half) * depth, depth), depth)
        block = router.at[my_group_rows, other]
        return pltpu.make_async_remote_copy(
            src_ref=block, dst_ref=block, send_sem=row_send.at[half + j], recv_sem=row_recv.at[half + j],
            device_id=(group, near_peer(j)), device_id_type=MESH,
        )

    def col_copy(j):
        return pltpu.make_async_remote_copy(
            src_ref=router.at[my_group_rows, :], dst_ref=router.at[my_group_rows, :],
            send_sem=col_send.at[j], recv_sem=col_recv.at[j],
            device_id=(group_peer(j), me), device_id_type=MESH,
        )

    start_load(0, 0)
    for place in range(RING):
        start_place(place)

    barrier = pltpu.get_barrier_semaphore()
    for j in range(1, members):
        pl.semaphore_signal(barrier, inc=1, device_id=(group, peer(j)), device_id_type=MESH)
    for j in range(1, groups):
        pl.semaphore_signal(barrier, inc=1, device_id=(group_peer(j), me), device_id_type=MESH)
    pl.semaphore_wait(barrier, members + groups - 2)

    def sums(step, slot):
        @pl.loop(0, members)
        def _(j):
            load(step, slot, j).wait()
            block = held[slot, j]
            partial[step, j] = jnp.sum(block * block, axis=0, keepdims=True)

        @pl.loop(1, members)
        def _(j):
            sum_copy(step, j).start()

    def total(step):
        @pl.loop(1, members)
        def _(j):
            sum_copy(step, j).wait_recv()

        value = partial[step, 0]
        for j in range(1, members):
            value = value + arrived[step, j]
        value = jnp.sqrt(value)
        scales[step, 0] = value
        index = step % local
        (scale_gate, scale_up)[step // local][index : index + 1, :] = value

        @pl.loop(1, members)
        def _(j):
            scale_copy(step, j).start()

    def scale_and_send(step, slot, reload):
        @pl.loop(1, members)
        def _(j):
            scale_copy(step, j).wait_recv()

        if step >= SLOTS:
            @pl.loop(1, members)
            def _(j):
                data_copy(step - SLOTS, j).wait_send()

        @pl.loop(1, members)
        def _(j):
            if reload:
                load(step, slot, j).wait()
            inverse = 1.0 / scales[step, lax.rem(members - j, members)]
            narrow[step % SLOTS, j] = (held[slot, j] * inverse).astype(jnp.bfloat16)

        @pl.loop(1, members)
        def _(j):
            data_copy(step, j).start()

        if reload:
            load(step, slot, 0).wait()
        _, final, index = source(step)
        own = held[slot, 0] * (1.0 / scales[step, 0])
        final[index, pl.ds(pl.multiple_of(me * rows, rows), rows), :] = own.astype(jnp.bfloat16)

    sums(0, 0)
    lead = min(SLOTS, steps)
    for step in range(1, lead):
        sums(step, 1 + (step - 1) % RING)
        start_place(step - 1 + RING)
    total(0)
    scale_and_send(0, 0, False)
    for step in range(lead, steps):
        sums(step, 1 + (step - 1) % RING)
        start_place(step - 1 + RING)
    for step in range(1, lead):
        total(step)

    router_own = pltpu.make_async_copy(part_router, my_block, router_sem.at[0])
    router_own.start()
    for j in near:
        row_copy(j).start()

    for step in range(1, steps):
        if step == 2:
            for late in range(lead, steps):
                total(late)
        place = steps - 2 + step
        scale_and_send(step, 1 + place % RING, True)
        start_place(place + RING)
        if step == steps // 2:
            for j in near:
                row_copy(j).wait()
            for j in range(1, members // 2):
                relay_copy(j).start()

    router_own.wait()
    for j in range(1, members // 2):
        relay_copy(j).wait()
    for j in range(1, groups):
        col_copy(j).start()

    for step in range(steps):
        @pl.loop(1, members)
        def _(j):
            sum_copy(step, j).wait_send()
            scale_copy(step, j).wait_send()
            data_copy(step, j).wait_recv()

        if step >= steps - SLOTS:
            @pl.loop(1, members)
            def _(j):
                data_copy(step, j).wait_send()

    for j in range(1, groups):
        col_copy(j).wait()


def exchange(groups, members, master_gate, master_up, part_router):
    experts, rows, inner = master_gate.shape
    local = experts // members
    steps = 2 * local
    width, depth = part_router.shape
    anywhere = pl.BlockSpec(memory_space=pl.ANY)
    in_vmem = pl.BlockSpec(memory_space=pltpu.VMEM)
    final = pltpu.VMEM((local, members * rows, inner), jnp.bfloat16)
    scale = jax.ShapeDtypeStruct((local, inner), jnp.float32)
    dma = pltpu.SemaphoreType.DMA
    return pl.pallas_call(
        functools.partial(kernel, groups, members, local, rows),
        out_shape=(
            final, final, scale, scale,
            jax.ShapeDtypeStruct((groups * width, members * depth), jnp.bfloat16),
        ),
        in_specs=[anywhere] * 3,
        out_specs=(in_vmem, in_vmem, in_vmem, in_vmem, anywhere),
        scratch_shapes=[
            pltpu.VMEM((1 + RING, members, rows, inner), jnp.float32),
            pltpu.VMEM((SLOTS, members, rows, inner), jnp.bfloat16),
            pltpu.VMEM((steps, members, 1, inner), jnp.float32),
            pltpu.VMEM((steps, members, 1, inner), jnp.float32),
            pltpu.VMEM((steps, members, 1, inner), jnp.float32),
            dma((1 + RING, members)),
            dma((steps, members)), dma((steps, members)),
            dma((steps, members)), dma((steps, members)),
            dma((steps, members)), dma((steps, members)),
            dma((members,)), dma((members,)), dma((groups,)), dma((groups,)), dma((1,)),
        ],
        compiler_params=pltpu.CompilerParams(
            collective_id=0, has_side_effects=True, vmem_limit_bytes=34 * 1024 * 1024
        ),
    )(master_gate, master_up, part_router)


def store_kernel(gate, up, final_gate, final_up, sem):
    copies = [
        pltpu.make_async_copy(landed.at[index], final.at[index], sem.at[which, index])
        for which, (landed, final) in enumerate(((gate, final_gate), (up, final_up)))
        for index in range(landed.shape[0])
    ]
    for copy in copies:
        copy.start()
    for copy in copies:
        copy.wait()


def store(gate, up):
    final = jax.ShapeDtypeStruct(gate.shape, gate.dtype)
    return pl.pallas_call(
        store_kernel,
        out_shape=(final, final),
        in_specs=[pl.BlockSpec(memory_space=pltpu.VMEM)] * 2,
        out_specs=(pl.BlockSpec(memory_space=pl.ANY),) * 2,
        scratch_shapes=[pltpu.SemaphoreType.DMA((2, gate.shape[0]))],
        compiler_params=pltpu.CompilerParams(vmem_limit_bytes=2 * 1024 * 1024),
    )(gate, up)


def solution(mesh):
    groups, members = mesh.shape["ep"], mesh.shape["fsdp"]

    def body(master_gate, master_up, router_weight, router_gain):
        part_router = (router_weight * router_gain[:, None]).astype(jnp.bfloat16).T
        final_gate, final_up, scale_gate, scale_up, router = exchange(
            groups, members, master_gate, master_up, part_router
        )
        final_gate, final_up = store(final_gate, final_up)
        return (final_gate, final_up, scale_gate, scale_up, router.T)

    return jax.shard_map(
        body,
        mesh=mesh,
        in_specs=(P("ep", "fsdp", None), P("ep", "fsdp", None), P("fsdp", "ep"), P("fsdp")),
        out_specs=(
            P(("ep", "fsdp"), None, None),
            P(("ep", "fsdp"), None, None),
            P(("ep", "fsdp"), None),
            P(("ep", "fsdp"), None),
            P(),
        ),
        check_vma=False,
    )
```

profile of v0, /device:TPU:12, one launch (start us, length us, event | category | flops | bytes accessed | tf_op | source)
XLA Modules:
  0.0 576.6 jit_solution(4308434766433284731)
XLA Ops:
  0.6 1.4 fusion.part_router
  2.0 563.8 %shard_map.83 = (bf16[4,2048,768]{2,1,0:T(8,128)(2,1)S(1)}, bf16[4,2048,768]{2,1,0:T(8,128)(2,1)S(1)}, f32[4,768]{1,0:T(4,128)}, f32[4,768]{1,0:T(4,128)}, bf16[128,2048]{1,0:T(8,128)(2,1)}) custom-call(f32[32,256,768]{2,1,0:T(8,128)} %gate.1, f32[32,256,768]{2,1,0:T(8,128)} %up.1, bf16[32,256]{1,0:T(8,128)(2,1)} %fusion.part_router), custom_call_target="tpu_custom_call" | custom-call | tf_op jit(solution)/shard_map/pallas_call | solution.py:240
  565.8 0.0 copy-start
  565.8 0.0 copy-start.2
  565.8 0.0 copy-start.1
  565.8 8.5 %shard_map.84 = (bf16[4,2048,768]{2,1,0:T(8,128)(2,1)}, bf16[4,2048,768]{2,1,0:T(8,128)(2,1)}) custom-call(bf16[4,2048,768]{2,1,0:T(8,128)(2,1)S(1)} %get-tuple-element.12.gate, bf16[4,2048,768]{2,1,0:T(8,128)(2,1)S(1)} %get-tuple-element.13.up), custom_call_target="tpu_custom_call" | custom-call | tf_op jit(solution)/shard_map/pallas_call | solution.py:280
  574.4 0.0 copy-done
  574.4 1.0 copy.9
  575.4 0.0 copy-done.2
  575.4 0.6 copy.12
  576.0 0.0 copy-done.1
  576.0 0.6 copy.13
Async XLA Ops:
  565.8 8.6 %copy-start = (bf16[128,2048]{1,0:T(8,128)(2,1)S(1)}, bf16[128,2048]{1,0:T(8,128)(2,1)}, u32[]{:S(2)}) copy-start(bf16[128,2048]{1,0:T(8,128)(2,1)} %get-tuple-element.18) | copy-start | bytes 1572868
  565.8 9.6 %copy-start.2 = (f32[4,768]{1,0:T(4,128)S(1)}, f32[4,768]{1,0:T(4,128)}, u32[]{:S(2)}) copy-start(f32[4,768]{1,0:T(4,128)} %get-tuple-element.31) | copy-start | bytes 36868
  565.8 10.2 %copy-start.1 = (f32[4,768]{1,0:T(4,128)S(1)}, f32[4,768]{1,0:T(4,128)}, u32[]{:S(2)}) copy-start(f32[4,768]{1,0:T(4,128)} %get-tuple-element.32) | copy-start | bytes 36868
where the time goes:
time: 577 us
  Pallas kernels  572 us (99%)
    pallas_call x1, Pallas kernels, exchange(): pl.pallas_call(functools.partial(kernel, groups, members, local, rows), o...  564 us

commit v1 on v0

v1 whole, which is shorter than its diff:
```python
import functools

import jax
import jax.numpy as jnp
from jax import lax
from jax.experimental import pallas as pl
from jax.experimental.pallas import tpu as pltpu
from jax.sharding import PartitionSpec as P

MESH = pl.DeviceIdType.MESH
RING = 2
SLOTS = 3
LANES = 128
UNITS = 8
GROUPS = ((0, 1), (1, 2), (3, 2), (5, 1), (6, 2))


def kernel(
    groups, members, local, rows,
    gate, up, weight, gain,
    final_gate, final_up, scale_gate, scale_up, serve,
    held, narrow, raw, stage,
    first, first_in, first_scales,
    late, near_in, far_in, total_far, far_total, scales,
    weight_in, gain_in, part_router, router,
    load_sem, send_sem, recv_sem, group_send, group_recv,
    first_send, first_recv, fscale_send, fscale_recv,
    raw_send, raw_recv, near_send, near_recv, cross_send, cross_recv,
    scale_send, scale_recv, relay_send, relay_recv,
    row_send, row_recv, col_send, col_recv, in_sem,
):
    group, me = lax.axis_index("ep"), lax.axis_index("fsdp")
    steps = 2 * local
    half = members // 2
    side, place_in_half = me // half, lax.rem(me, half)
    unit = rows // UNITS

    def peer(j):
        return lax.rem(me + j, members)

    def back(j):
        return lax.rem(me + members - j, members)

    def near_peer(n):
        return side * half + lax.rem(place_in_half + n, half)

    def far_peer(n):
        return (1 - side) * half + lax.rem(place_in_half + n, half)

    def offset(device):
        return lax.rem(device + members - me, members)

    def is_far(device):
        return device // half != side

    def group_peer(j):
        return lax.rem(group + j, groups)

    def remote(source, target, send, recv, member):
        return pltpu.make_async_remote_copy(
            src_ref=source, dst_ref=target, send_sem=send, recv_sem=recv,
            device_id=(group, member), device_id_type=MESH,
        )

    def source(step):
        return (gate, up)[step // local], (final_gate, final_up)[step // local], step % local

    order = [*range(1, steps), *range(1, steps)]

    def load(step, slot, j):
        master, _, index = source(step)
        return pltpu.make_async_copy(
            master.at[peer(j) * local + index], held.at[slot, j], load_sem.at[slot, j]
        )

    def start_load(step, slot):
        @pl.loop(0, members)
        def _(j):
            load(step, slot, j).start()

    def start_place(place):
        if place < len(order):
            start_load(order[place], 1 + place % RING)

    def rows_of(member):
        return pl.ds(pl.multiple_of(member * rows, rows), rows)

    def data_copy(step, j):
        _, final, index = source(step)
        return remote(
            narrow.at[step % SLOTS, j], final.at[index, rows_of(me), :],
            send_sem.at[step, j], recv_sem.at[step, j], peer(j),
        )

    def group_copy(g, j, far):
        begin, count = GROUPS[g]
        begin, count = begin * unit, count * unit
        there = pl.ds(pl.multiple_of(me * rows + begin, unit), count)
        columns = slice(LANES, None) if far else slice(None)
        return remote(
            narrow.at[0, j, begin : begin + count, columns], final_gate.at[0, there, columns],
            group_send.at[g, j], group_recv.at[g, j], peer(j),
        )

    def each_group_copy(g, sending, act):
        @pl.loop(1, members)
        def _(j):
            other = peer(j) if sending else back(j)

            @pl.when(is_far(other))
            def _():
                act(group_copy(g, j, True))

            @pl.when(jnp.logical_not(is_far(other)))
            def _():
                act(group_copy(g, j, False))

    def first_copy(j):
        return remote(first.at[j], first_in.at[j], first_send.at[j], first_recv.at[j], peer(j))

    def first_scale_copy(j):
        return remote(
            first_scales.at[0], first_scales.at[j], fscale_send.at[j], fscale_recv.at[j], peer(j)
        )

    def raw_copy(piece, n):
        count = rows // 2
        part = slice(piece * count, (piece + 1) * count)
        return remote(
            raw.at[n, part, :], stage.at[n, part, :],
            raw_send.at[piece, n], raw_recv.at[piece, n], far_peer(n),
        )

    def near_copy(n, far):
        owner = far_peer(n) if far else near_peer(n)
        return remote(
            late.at[offset(owner)], (far_in if far else near_in).at[n],
            near_send.at[int(far), n], near_recv.at[int(far), n], near_peer(n),
        )

    def cross_copy():
        return remote(total_far, far_total, cross_send.at[0], cross_recv.at[0], far_peer(0))

    def scale_copy(n):
        return remote(scales.at[0], scales.at[n], scale_send.at[n], scale_recv.at[n], near_peer(n))

    def far_scale_copy():
        return remote(
            scales.at[0], scales.at[half], scale_send.at[0], scale_recv.at[0], far_peer(0)
        )

    def relay_scale_copy(n):
        return remote(
            scales.at[half], scales.at[half + n], relay_send.at[n], relay_recv.at[n], near_peer(n)
        )

    def scale_slot(device):
        n = lax.rem(place_in_half + half - lax.rem(device, half), half)
        return jnp.where(is_far(device), half, 0) + n

    width, depth = part_router.shape
    my_group_rows = pl.ds(pl.multiple_of(group * width, width), width)
    my_columns = pl.ds(pl.multiple_of(me * depth, depth), depth)
    near = [*range(1, half), half]

    def row_peer(j):
        return far_peer(0) if j == half else near_peer(j)

    def row_copy(j):
        return remote(
            part_router, router.at[my_group_rows, my_columns],
            row_send.at[j], row_recv.at[j], row_peer(j),
        )

    def relay_copy(j):
        other = pl.ds(pl.multiple_of(far_peer(0) * depth, depth), depth)
        block = router.at[my_group_rows, other]
        return remote(block, block, row_send.at[half + j], row_recv.at[half + j], near_peer(j))

    def col_copy(j):
        return pltpu.make_async_remote_copy(
            src_ref=router.at[my_group_rows, :], dst_ref=router.at[my_group_rows, :],
            send_sem=col_send.at[j], recv_sem=col_recv.at[j],
            device_id=(group_peer(j), me), device_id_type=MESH,
        )

    barrier = pltpu.get_barrier_semaphore()
    for j in range(1, members):
        pl.semaphore_signal(barrier, inc=1, device_id=(group, peer(j)), device_id_type=MESH)
    for j in range(1, groups):
        pl.semaphore_signal(barrier, inc=1, device_id=(group_peer(j), me), device_id_type=MESH)

    start_load(0, 0)
    for place in range(RING):
        start_place(place)
    weight_copy = pltpu.make_async_copy(weight, weight_in, in_sem.at[0])
    gain_copy = pltpu.make_async_copy(gain, gain_in, in_sem.at[1])
    weight_copy.start()
    gain_copy.start()

    def sums(step, slot):
        @pl.loop(0, members)
        def _(j):
            load(step, slot, j).wait()
            block = held[slot, j]
            value = jnp.sum(block * block, axis=0, keepdims=True)
            if step == 0:
                first[j] = value
            else:
                late[j, step - 1] = value

    def late_sums(begin, end):
        for step in range(begin, min(end, steps)):
            sums(step, 1 + (step - 1) % RING)
            start_place(step - 1 + RING)

    def finish(step, value):
        index = step % local
        (scale_gate, scale_up)[step // local][index : index + 1, :] = value

    def keep_own(step, slot, inverse):
        _, final, index = source(step)
        final[index, rows_of(me), :] = (held[slot, 0] * inverse).astype(jnp.bfloat16)

    sums(0, 0)

    pl.semaphore_wait(barrier, members + groups - 2)

    @pl.loop(1, members)
    def _(j):
        first_copy(j).start()

    @pl.loop(0, half)
    def _(n):
        raw[n] = held[0, offset(far_peer(n)), :, 0:LANES].astype(jnp.bfloat16)

    @pl.loop(0, half)
    def _(n):
        raw_copy(0, n).start()

    late_sums(1, 3)

    @pl.loop(1, members)
    def _(j):
        first_copy(j).wait_recv()

    value = first[0]
    for j in range(1, members):
        value = value + first_in[j]
    value = jnp.sqrt(value)
    first_scales[0] = value
    finish(0, value)

    @pl.loop(1, members)
    def _(j):
        first_scale_copy(j).start()

    @pl.loop(0, half)
    def _(n):
        raw_copy(1, n).start()

    late_sums(3, 6)

    @pl.loop(1, members)
    def _(j):
        first_scale_copy(j).wait_recv()

    @pl.loop(1, members)
    def _(j):
        inverse = 1.0 / first_scales[lax.rem(members - j, members)]
        narrow[0, j] = (held[0, j] * inverse).astype(jnp.bfloat16)

    def start_group(g):
        each_group_copy(g, True, lambda copy: copy.start())

    start_group(0)

    late_sums(6, steps)

    for n in range(1, half):
        for far in (True, False):
            near_copy(n, far).start()

    start_group(1)

    my_inverse = 1.0 / first_scales[0]
    keep_own(0, 0, my_inverse)

    weight_copy.wait()
    gain_copy.wait()
    part_router[...] = (weight_in[...] * gain_in[...]).astype(jnp.bfloat16)
    router[my_group_rows, my_columns] = part_router[...]

    @pl.loop(0, half)
    def _(n):
        for piece in range(2):
            raw_copy(piece, n).wait_recv()
        from_member = (1 - side) * half + lax.rem(place_in_half + half - n, half)
        block = stage[n].astype(jnp.float32) * my_inverse[:, 0:LANES]
        final_gate[0, rows_of(from_member), 0:LANES] = block.astype(jnp.bfloat16)

    for n in range(1, half):
        for far in (True, False):
            near_copy(n, far).wait_recv()
    gathered = late[half]
    for n in range(1, half):
        gathered = gathered + far_in[n]
    total_far[...] = gathered
    cross_copy().start()

    start_group(2)

    gathered = late[0]
    for n in range(1, half):
        gathered = gathered + near_in[n]
    cross_copy().wait_recv()
    scales[0] = jnp.sqrt(gathered + far_total[...])
    far_scale_copy().start()
    for n in range(1, half):
        scale_copy(n).start()

    start_group(3)

    for step in range(1, steps):
        finish(step, scales[0, step - 1])

    far_scale_copy().wait_recv()
    for n in range(1, half):
        relay_scale_copy(n).start()

    start_group(4)

    for j in near:
        row_copy(j).start()

    for n in range(1, half):
        scale_copy(n).wait_recv()
        relay_scale_copy(n).wait_recv()

    def wait_sent(step):
        if step == 0:
            for g in range(len(GROUPS)):
                each_group_copy(g, True, lambda copy: copy.wait_send())
        else:
            @pl.loop(1, members)
            def _(j):
                data_copy(step, j).wait_send()

    def scale_and_send(step, slot):
        if step >= SLOTS:
            wait_sent(step - SLOTS)

        @pl.loop(1, members)
        def _(j):
            load(step, slot, j).wait()
            inverse = 1.0 / scales[scale_slot(peer(j)), step - 1]
            narrow[step % SLOTS, j] = (held[slot, j] * inverse).astype(jnp.bfloat16)

        @pl.loop(1, members)
        def _(j):
            data_copy(step, j).start()

        load(step, slot, 0).wait()
        keep_own(step, slot, 1.0 / scales[0, step - 1])

    for step in range(1, steps):
        place = steps - 2 + step
        scale_and_send(step, 1 + place % RING)
        start_place(place + RING)
        if step == steps // 2:
            for j in near:
                row_copy(j).wait()
            for j in range(1, half):
                relay_copy(j).start()

    for j in range(1, half):
        relay_copy(j).wait()
    for j in range(1, groups):
        col_copy(j).start()

    @pl.loop(1, members)
    def _(j):
        first_copy(j).wait_send()
        first_scale_copy(j).wait_send()

    @pl.loop(0, half)
    def _(n):
        for piece in range(2):
            raw_copy(piece, n).wait_send()

    for n in range(1, half):
        for far in (True, False):
            near_copy(n, far).wait_send()
        scale_copy(n).wait_send()
        relay_scale_copy(n).wait_send()
    cross_copy().wait_send()
    far_scale_copy().wait_send()

    for j in range(1, groups):
        col_copy(j).wait()

    @pl.loop(0, router.shape[1] // LANES)
    def _(block):
        here = pl.ds(pl.multiple_of(block * LANES, LANES), LANES)
        serve[here, :] = router[:, here].astype(jnp.float32).T.astype(jnp.bfloat16)

    for step in range(steps):
        if step >= steps - SLOTS:
            wait_sent(step)
        if step == 0:
            for g in range(len(GROUPS)):
                each_group_copy(g, False, lambda copy: copy.wait_recv())
        else:
            @pl.loop(1, members)
            def _(j):
                data_copy(step, j).wait_recv()


def exchange(groups, members, master_gate, master_up, weight, gain):
    experts, rows, inner = master_gate.shape
    local = experts // members
    steps = 2 * local
    half = members // 2
    width, depth = weight.shape
    in_hbm = pl.BlockSpec(memory_space=pltpu.HBM)
    in_vmem = pl.BlockSpec(memory_space=pltpu.VMEM)
    final = pltpu.VMEM((local, members * rows, inner), jnp.bfloat16)
    scale = pltpu.VMEM((local, inner), jnp.float32)
    dma = pltpu.SemaphoreType.DMA

    def sums(*shape):
        return pltpu.VMEM((*shape, 1, inner), jnp.float32)

    late = steps - 1
    return pl.pallas_call(
        functools.partial(kernel, groups, members, local, rows),
        out_shape=(
            final, final, scale, scale,
            pltpu.VMEM((members * depth, groups * width), jnp.bfloat16),
        ),
        in_specs=[in_hbm] * 4,
        out_specs=(in_vmem,) * 5,
        scratch_shapes=[
            pltpu.VMEM((1 + RING, members, rows, inner), jnp.float32),
            pltpu.VMEM((SLOTS, members, rows, inner), jnp.bfloat16),
            pltpu.VMEM((half, rows, LANES), jnp.bfloat16),
            pltpu.VMEM((half, rows, LANES), jnp.bfloat16),
            sums(members), sums(members), sums(members),
            sums(members, late), sums(half, late), sums(half, late),
            sums(late), sums(late), sums(members, late),
            pltpu.VMEM((width, depth), jnp.float32),
            pltpu.VMEM((1, depth), jnp.float32),
            pltpu.VMEM((width, depth), jnp.bfloat16),
            pltpu.VMEM((groups * width, members * depth), jnp.bfloat16),
            dma((1 + RING, members)),
            dma((steps, members)), dma((steps, members)),
            dma((len(GROUPS), members)), dma((len(GROUPS), members)),
            dma((members,)), dma((members,)), dma((members,)), dma((members,)),
            dma((2, half)), dma((2, half)), dma((2, half)), dma((2, half)), dma((1,)), dma((1,)),
            dma((half,)), dma((half,)), dma((half,)), dma((half,)),
            dma((members,)), dma((members,)), dma((groups,)), dma((groups,)), dma((2,)),
        ],
        compiler_params=pltpu.CompilerParams(
            collective_id=0, has_side_effects=True, vmem_limit_bytes=35 * 1024 * 1024
        ),
    )(master_gate, master_up, weight, gain)


def store_kernel(*refs):
    count = (len(refs) - 1) // 2
    sem = refs[-1]
    copies = []
    for landed, stored in zip(refs[:count], refs[count:-1]):
        if len(landed.shape) == 3:
            pairs = [(landed.at[i], stored.at[i]) for i in range(landed.shape[0])]
        else:
            pairs = [(landed, stored)]
        for here, there in pairs:
            copies.append(pltpu.make_async_copy(here, there, sem.at[len(copies)]))
    for copy in copies:
        copy.start()
    for copy in copies:
        copy.wait()


def store(*landed):
    pieces = sum(array.shape[0] if array.ndim == 3 else 1 for array in landed)
    return pl.pallas_call(
        store_kernel,
        out_shape=tuple(jax.ShapeDtypeStruct(array.shape, array.dtype) for array in landed),
        in_specs=[pl.BlockSpec(memory_space=pltpu.VMEM)] * len(landed),
        out_specs=(pl.BlockSpec(memory_space=pl.ANY),) * len(landed),
        scratch_shapes=[pltpu.SemaphoreType.DMA((pieces,))],
        compiler_params=pltpu.CompilerParams(vmem_limit_bytes=2 * 1024 * 1024),
    )(*landed)


def solution(mesh):
    groups, members = mesh.shape["ep"], mesh.shape["fsdp"]

    def body(master_gate, master_up, router_weight, router_gain):
        landed = exchange(
            groups, members, master_gate, master_up, router_weight.T, router_gain[None, :]
        )
        return store(*landed)

    return jax.shard_map(
        body,
        mesh=mesh,
        in_specs=(P("ep", "fsdp", None), P("ep", "fsdp", None), P("fsdp", "ep"), P("fsdp")),
        out_specs=(
            P(("ep", "fsdp"), None, None),
            P(("ep", "fsdp"), None, None),
            P(("ep", "fsdp"), None),
            P(("ep", "fsdp"), None),
            P(),
        ),
        check_vma=False,
    )
```

time: 577 us -> 561 us (0.972)
  Pallas kernels: 572 us -> 560 us
    pallas_call x1, Pallas kernels: 564 us -> 551 us  [exchange(): pl.pallas_call(functools.partial(kernel, groups, members, local, rows), o...]
where the time goes in v1:
time: 561 us
  Pallas kernels  560 us (100%)
    pallas_call x1, Pallas kernels, exchange(): pl.pallas_call(functools.partial(kernel, groups, members, local, rows), o...  551 us

profile of v1, /device:TPU:12, one launch (start us, length us, event | category | flops | bytes accessed | tf_op | source)
XLA Modules:
  0.0 560.7 jit_solution(18096279827194100279)
XLA Ops:
  0.6 551.4 %shard_map.83 = (bf16[4,2048,768]{2,1,0:T(8,128)(2,1)S(1)}, bf16[4,2048,768]{2,1,0:T(8,128)(2,1)S(1)}, f32[4,768]{1,0:T(4,128)S(1)}, f32[4,768]{1,0:T(4,128)S(1)}, bf16[2048,128]{1,0:T(8,128)(2,1)S(1)}) custom-call(f32[32,256,768]{2,1,0:T(8,128)} %gate.1, f32[32,256,768]{2,1,0:T(8,128)} %up.1, f32[32,256]{1,0:T(8,128)} %bitcast.2, f32[1,256]{1,0:T(1,128)} %bitcast.3), custom_call_target="tpu_custom_call" | custom-call | tf_op jit(solution)/shard_map/pallas_call | solution.py:435
  552.1 8.6 %shard_map.84 = (bf16[4,2048,768]{2,1,0:T(8,128)(2,1)}, bf16[4,2048,768]{2,1,0:T(8,128)(2,1)}, f32[4,768]{1,0:T(4,128)}, f32[4,768]{1,0:T(4,128)}, bf16[2048,128]{1,0:T(8,128)(2,1)}) custom-call(bf16[4,2048,768]{2,1,0:T(8,128)(2,1)S(1)} %get-tuple-element.10.refs_0_, bf16[4,2048,768]{2,1,0:T(8,128)(2,1)S(1)} %get-tuple-element.11.refs_1_, ...), custom_call_target="tpu_custom_call" | custom-call | tf_op jit(solution)/shard_map/pallas_call | solution.py:488

commit v2 on v1

--- a/solution.py
+++ b/solution.py
@@ -13,12 +13,21 @@
 LANES = 128
 UNITS = 8
 GROUPS = ((0, 1), (1, 2), (3, 2), (5, 1), (6, 2))
+KEPT_UNITS = 6
+
+
+def in_middle(member, members):
+    return jnp.logical_and(member >= members // 4, member < members - members // 4)
+
+
+def partner_of(member, members):
+    return jnp.where(member < members // 2, member + members // 4, member - members // 4)
 
 
 def kernel(
     groups, members, local, rows,
     gate, up, weight, gain,
-    final_gate, final_up, scale_gate, scale_up, serve,
+    final_gate, final_up, scale_gate, scale_up, serve, kept,
     held, narrow, raw, stage,
     first, first_in, first_scales,
     late, near_in, far_in, total_far, far_total, scales,
@@ -92,6 +101,36 @@
             send_sem.at[step, j], recv_sem.at[step, j], peer(j),
         )
 
+    kept_rows = KEPT_UNITS * unit
+    partner = partner_of(me, members)
+
+    def short_copy(j):
+        step = steps - 1
+        count = rows - kept_rows
+        there = pl.ds(pl.multiple_of(me * rows, rows), count)
+        return remote(
+            narrow.at[step % SLOTS, j, 0:count], final_up.at[local - 1, there, :],
+            send_sem.at[step, j], recv_sem.at[step, j], peer(j),
+        )
+
+    def each_data_copy(step, sending, act):
+        @pl.loop(1, members)
+        def _(j):
+            if step < steps - 1:
+                act(data_copy(step, j))
+            else:
+                other = peer(j) if sending else back(j)
+                short = jnp.logical_and(in_middle(me, members), other == partner)
+
+                @pl.when(jnp.logical_not(short))
+                def _():
+                    act(data_copy(step, j))
+
+                if kept_rows < rows:
+                    @pl.when(short)
+                    def _():
+                        act(short_copy(j))
+
     def group_copy(g, j, far):
         begin, count = GROUPS[g]
         begin, count = begin * unit, count * unit
@@ -342,9 +381,7 @@
             for g in range(len(GROUPS)):
                 each_group_copy(g, True, lambda copy: copy.wait_send())
         else:
-            @pl.loop(1, members)
-            def _(j):
-                data_copy(step, j).wait_send()
+            each_data_copy(step, True, lambda copy: copy.wait_send())
 
     def scale_and_send(step, slot):
         if step >= SLOTS:
@@ -356,9 +393,9 @@
             inverse = 1.0 / scales[scale_slot(peer(j)), step - 1]
             narrow[step % SLOTS, j] = (held[slot, j] * inverse).astype(jnp.bfloat16)
 
-        @pl.loop(1, members)
-        def _(j):
-            data_copy(step, j).start()
+        each_data_copy(step, True, lambda copy: copy.start())
+        if step == steps - 1:
+            kept[...] = narrow[step % SLOTS, offset(partner), rows - kept_rows :]
 
         load(step, slot, 0).wait()
         keep_own(step, slot, 1.0 / scales[0, step - 1])
@@ -411,9 +448,7 @@
             for g in range(len(GROUPS)):
                 each_group_copy(g, False, lambda copy: copy.wait_recv())
         else:
-            @pl.loop(1, members)
-            def _(j):
-                data_copy(step, j).wait_recv()
+            each_data_copy(step, False, lambda copy: copy.wait_recv())
 
 
 def exchange(groups, members, master_gate, master_up, weight, gain):
@@ -437,9 +472,10 @@
         out_shape=(
             final, final, scale, scale,
             pltpu.VMEM((members * depth, groups * width), jnp.bfloat16),
+            pltpu.VMEM((rows // UNITS * KEPT_UNITS, inner), jnp.bfloat16),
         ),
         in_specs=[in_hbm] * 4,
-        out_specs=(in_vmem,) * 5,
+        out_specs=(in_vmem,) * 6,
         scratch_shapes=[
             pltpu.VMEM((1 + RING, members, rows, inner), jnp.float32),
             pltpu.VMEM((SLOTS, members, rows, inner), jnp.bfloat16),
@@ -490,19 +526,52 @@
         out_shape=tuple(jax.ShapeDtypeStruct(array.shape, array.dtype) for array in landed),
         in_specs=[pl.BlockSpec(memory_space=pltpu.VMEM)] * len(landed),
         out_specs=(pl.BlockSpec(memory_space=pl.ANY),) * len(landed),
+        cost_estimate=pl.CostEstimate(flops=20_000_000, bytes_accessed=1000, transcendentals=0),
         scratch_shapes=[pltpu.SemaphoreType.DMA((pieces,))],
         compiler_params=pltpu.CompilerParams(vmem_limit_bytes=2 * 1024 * 1024),
     )(*landed)
 
 
+def place_kernel(members, rows, moved, whole, placed, sem):
+    del whole
+    me = lax.axis_index("fsdp")
+    count = moved.shape[0]
+
+    @pl.when(in_middle(me, members))
+    def _():
+        begin = partner_of(me, members) * rows + (rows - count)
+        there = pl.ds(pl.multiple_of(begin, rows // UNITS), count)
+        copy = pltpu.make_async_copy(moved, placed.at[placed.shape[0] - 1, there, :], sem.at[0])
+        copy.start()
+        copy.wait()
+
+
+def place(members, rows, moved, whole):
+    anywhere = pl.BlockSpec(memory_space=pl.ANY)
+    return pl.pallas_call(
+        functools.partial(place_kernel, members, rows),
+        out_shape=jax.ShapeDtypeStruct(whole.shape, whole.dtype),
+        in_specs=[pl.BlockSpec(memory_space=pltpu.VMEM), anywhere],
+        out_specs=anywhere,
+        input_output_aliases={1: 0},
+        scratch_shapes=[pltpu.SemaphoreType.DMA((1,))],
+        compiler_params=pltpu.CompilerParams(vmem_limit_bytes=2 * 1024 * 1024),
+    )(moved, whole)
+
+
 def solution(mesh):
     groups, members = mesh.shape["ep"], mesh.shape["fsdp"]
 
     def body(master_gate, master_up, router_weight, router_gain):
-        landed = exchange(
+        *landed, kept = exchange(
             groups, members, master_gate, master_up, router_weight.T, router_gain[None, :]
         )
-        return store(*landed)
+        low = range(members // 4, members // 2)
+        pairs = [(i, i + members // 4) for i in low] + [(i + members // 4, i) for i in low]
+        moved = lax.ppermute(kept, "fsdp", pairs)
+        final_gate, final_up, *rest = store(*landed)
+        final_up = place(members, master_gate.shape[1], moved, final_up)
+        return (final_gate, final_up, *rest)
 
     return jax.shard_map(
         body,

time: 561 us -> 558 us (level)
  Pallas kernels: 560 us -> 554 us
    pallas_call x1, Pallas kernels: 551 us -> 545 us  [exchange(): pl.pallas_call(functools.partial(kernel, groups, members, local, rows), o...]
  transfers between devices with their start and end apart: 0 -> 1, of which waited for: 0 -> 0; matrix products, arithmetic and copies ran while one was open for 0% -> 0% of each run, Pallas kernels for 0% -> 2%
where the time goes in v2:
time: 558 us; the launch traced here: 557 us
  Pallas kernels  554 us (99%)
    pallas_call x1, Pallas kernels, exchange(): pl.pallas_call(functools.partial(kernel, groups, members, local, rows), o...  545 us
  transfers between devices with their start and end apart: 1, of which 0 were waited for; matrix products, arithmetic and copies ran while one was open for 0% of the time, Pallas kernels for 2%

profile of v2, /device:TPU:12, one launch (start us, length us, event | category | flops | bytes accessed | tf_op | source)
XLA Modules:
  0.0 557.1 jit_solution(8297484444148908878)
XLA Ops:
  0.6 545.1 %shard_map.83 = (bf16[4,2048,768]{2,1,0:T(8,128)(2,1)S(1)}, bf16[4,2048,768]{2,1,0:T(8,128)(2,1)S(1)}, f32[4,768]{1,0:T(4,128)S(1)}, f32[4,768]{1,0:T(4,128)S(1)...) custom-call(f32[32,256,768]{2,1,0:T(8,128)} %gate.1, f32[32,256,768]{2,1,0:T(8,128)} %up.1, ...), custom_call_target="tpu_custom_call" | custom-call | tf_op jit(solution)/shard_map/pallas_call | solution.py:470
  545.8 1.9 collective-permute-start
  547.7 8.6 %shard_map.84 = (bf16[4,2048,768]{2,1,0:T(8,128)(2,1)}, bf16[4,2048,768]{2,1,0:T(8,128)(2,1)}, f32[4,768]{1,0:T(4,128)}, f32[4,768]{1,0:T(4,128)}, bf16[2048,128]{1,0:T(8,128)(2,1)}) custom-call(bf16[4,2048,768]{2,1,0:T(8,128)(2,1)S(1)} %get-tuple-element.16.refs_0_, bf16[4,2048,768]{2,1,0:T(8,128)(2,1)S(1)} %get-tuple-element.17.refs_1_, ...), custom_call_target="tpu_custom_call" | custom-call | flops 20000000 | bytes 1000 | tf_op jit(solution)/shard_map/pallas_call | solution.py:524
  556.3 0.0 collective-permute-done.moved
  556.3 0.7 shard_map.85
Async XLA Ops:
  545.8 10.6 %collective-permute-start = (bf16[192,768]{1,0:T(8,128)(2,1)S(1)}, bf16[192,768]{1,0:T(8,128)(2,1)S(1)}, u32[]{:S(2)}, u32[]{:S(2)}) collective-permute-start(bf16[192,768]{1,0:T(8,128)(2,1)S(1)} %get-tuple-element.22), channel_id=1, source_target_pairs={{2,4},{3,5},{4,2},{5,3},{10,12},{11,13},{12,10},{13,11},{18,20},{1... | collective-permute-start | bytes 884744 | tf_op jit(solution)/shard_map/ppermute | solution.py:571

commit v3 on v2

--- a/solution.py
+++ b/solution.py
@@ -13,11 +13,17 @@
 LANES = 128
 UNITS = 8
 GROUPS = ((0, 1), (1, 2), (3, 2), (5, 1), (6, 2))
-KEPT_UNITS = 6
-
-
-def in_middle(member, members):
-    return jnp.logical_and(member >= members // 4, member < members - members // 4)
+KEPT_UNITS = (8, 8, 4)
+
+
+def takes_part(group, member, members):
+    middle = jnp.logical_and(member >= members // 4, member < members - members // 4)
+    return jnp.logical_and(middle, lax.rem(group, 2) == 1)
+
+
+def kept_rows_of(local, rows):
+    unit = rows // UNITS
+    return {2 * local - 1 - i: count * unit for i, count in enumerate(KEPT_UNITS[:local])}
 
 
 def partner_of(member, members):
@@ -101,35 +107,35 @@
             send_sem.at[step, j], recv_sem.at[step, j], peer(j),
         )
 
-    kept_rows = KEPT_UNITS * unit
+    kept_rows = kept_rows_of(local, rows)
     partner = partner_of(me, members)
 
-    def short_copy(j):
-        step = steps - 1
-        count = rows - kept_rows
+    def short_copy(step, j):
+        count = rows - kept_rows[step]
+        _, final, index = source(step)
         there = pl.ds(pl.multiple_of(me * rows, rows), count)
         return remote(
-            narrow.at[step % SLOTS, j, 0:count], final_up.at[local - 1, there, :],
+            narrow.at[step % SLOTS, j, 0:count], final.at[index, there, :],
             send_sem.at[step, j], recv_sem.at[step, j], peer(j),
         )
 
     def each_data_copy(step, sending, act):
         @pl.loop(1, members)
         def _(j):
-            if step < steps - 1:
+            if step not in kept_rows:
                 act(data_copy(step, j))
             else:
                 other = peer(j) if sending else back(j)
-                short = jnp.logical_and(in_middle(me, members), other == partner)
+                short = jnp.logical_and(takes_part(group, me, members), other == partner)
 
                 @pl.when(jnp.logical_not(short))
                 def _():
                     act(data_copy(step, j))
 
-                if kept_rows < rows:
+                if kept_rows[step] < rows:
                     @pl.when(short)
                     def _():
-                        act(short_copy(j))
+                        act(short_copy(step, j))
 
     def group_copy(g, j, far):
         begin, count = GROUPS[g]
@@ -394,8 +400,10 @@
             narrow[step % SLOTS, j] = (held[slot, j] * inverse).astype(jnp.bfloat16)
 
         each_data_copy(step, True, lambda copy: copy.start())
-        if step == steps - 1:
-            kept[...] = narrow[step % SLOTS, offset(partner), rows - kept_rows :]
+        if step in kept_rows:
+            count = kept_rows[step]
+            begin = sum(size for other, size in kept_rows.items() if other > step)
+            kept[begin : begin + count] = narrow[step % SLOTS, offset(partner), rows - count :]
 
         load(step, slot, 0).wait()
         keep_own(step, slot, 1.0 / scales[0, step - 1])
@@ -472,7 +480,7 @@
         out_shape=(
             final, final, scale, scale,
             pltpu.VMEM((members * depth, groups * width), jnp.bfloat16),
-            pltpu.VMEM((rows // UNITS * KEPT_UNITS, inner), jnp.bfloat16),
+            pltpu.VMEM((sum(kept_rows_of(local, rows).values()), inner), jnp.bfloat16),
         ),
         in_specs=[in_hbm] * 4,
         out_specs=(in_vmem,) * 6,
@@ -534,16 +542,26 @@
 
 def place_kernel(members, rows, moved, whole, placed, sem):
     del whole
-    me = lax.axis_index("fsdp")
-    count = moved.shape[0]
-
-    @pl.when(in_middle(me, members))
+    group, me = lax.axis_index("ep"), lax.axis_index("fsdp")
+    local = placed.shape[0]
+
+    @pl.when(takes_part(group, me, members))
     def _():
-        begin = partner_of(me, members) * rows + (rows - count)
-        there = pl.ds(pl.multiple_of(begin, rows // UNITS), count)
-        copy = pltpu.make_async_copy(moved, placed.at[placed.shape[0] - 1, there, :], sem.at[0])
-        copy.start()
-        copy.wait()
+        copies, begin = [], 0
+        for step, count in kept_rows_of(local, rows).items():
+            first = partner_of(me, members) * rows + (rows - count)
+            there = pl.ds(pl.multiple_of(first, rows // UNITS), count)
+            copies.append(
+                pltpu.make_async_copy(
+                    moved.at[begin : begin + count], placed.at[step - local, there, :],
+                    sem.at[len(copies)],
+                )
+            )
+            begin += count
+        for copy in copies:
+            copy.start()
+        for copy in copies:
+            copy.wait()
 
 
 def place(members, rows, moved, whole):
@@ -554,7 +572,7 @@
         in_specs=[pl.BlockSpec(memory_space=pltpu.VMEM), anywhere],
         out_specs=anywhere,
         input_output_aliases={1: 0},
-        scratch_shapes=[pltpu.SemaphoreType.DMA((1,))],
+        scratch_shapes=[pltpu.SemaphoreType.DMA((len(KEPT_UNITS),))],
         compiler_params=pltpu.CompilerParams(vmem_limit_bytes=2 * 1024 * 1024),
     )(moved, whole)
 
@@ -566,9 +584,13 @@
         *landed, kept = exchange(
             groups, members, master_gate, master_up, router_weight.T, router_gain[None, :]
         )
-        low = range(members // 4, members // 2)
+        low = [
+            g * members + i
+            for g in range(1, groups, 2)
+            for i in range(members // 4, members // 2)
+        ]
         pairs = [(i, i + members // 4) for i in low] + [(i + members // 4, i) for i in low]
-        moved = lax.ppermute(kept, "fsdp", pairs)
+        moved = lax.ppermute(kept, ("ep", "fsdp"), pairs)
         final_gate, final_up, *rest = store(*landed)
         final_up = place(members, master_gate.shape[1], moved, final_up)
         return (final_gate, final_up, *rest)

time: 558 us -> 555 us (level)
  no operation moved by 1% of the time
where the time goes in v3:
time: 555 us
  Pallas kernels  554 us (100%)
    pallas_call x1, Pallas kernels, exchange(): pl.pallas_call(functools.partial(kernel, groups, members, local, rows), o...  545 us
  transfers between devices with their start and end apart: 1, of which 0 were waited for; matrix products, arithmetic and copies ran while one was open for 0% of the time, Pallas kernels for 2%

profile of v3, /device:TPU:12, one launch (start us, length us, event | category | flops | bytes accessed | tf_op | source)
XLA Modules:
  0.0 555.1 jit_solution(4952406178505237106)
XLA Ops:
  0.6 545.0 %shard_map.83 = (bf16[4,2048,768]{2,1,0:T(8,128)(2,1)S(1)}, bf16[4,2048,768]{2,1,0:T(8,128)(2,1)S(1)}, f32[4,768]{1,0:T(4,128)S(1)}, f32[4,768]{1,0:T(4,128)S(1)...) custom-call(f32[32,256,768]{2,1,0:T(8,128)} %gate.1, f32[32,256,768]{2,1,0:T(8,128)} %up.1, ...), custom_call_target="tpu_custom_call" | custom-call | tf_op jit(solution)/shard_map/pallas_call | solution.py:478
  545.7 0.7 collective-permute-start
  546.4 8.6 %shard_map.84 = (bf16[4,2048,768]{2,1,0:T(8,128)(2,1)}, bf16[4,2048,768]{2,1,0:T(8,128)(2,1)}, f32[4,768]{1,0:T(4,128)}, f32[4,768]{1,0:T(4,128)}, bf16[2048,128]{1,0:T(8,128)(2,1)}) custom-call(bf16[4,2048,768]{2,1,0:T(8,128)(2,1)S(1)} %get-tuple-element.16.refs_0_, bf16[4,2048,768]{2,1,0:T(8,128)(2,1)S(1)} %get-tuple-element.17.refs_1_, ...), custom_call_target="tpu_custom_call" | custom-call | flops 20000000 | bytes 1000 | tf_op jit(solution)/shard_map/pallas_call | solution.py:532
  555.1 0.0 collective-permute-done.moved
  555.1 0.1 shard_map.85
Async XLA Ops:
  545.7 9.4 %collective-permute-start = (bf16[640,768]{1,0:T(8,128)(2,1)S(1)}, bf16[640,768]{1,0:T(8,128)(2,1)S(1)}, u32[]{:S(2)}, u32[]{:S(2)}) collective-permute-start(bf16[640,768]{1,0:T(8,128)(2,1)S(1)} %get-tuple-element.22), channel_id=1, source_target_pairs={{10,12},{11,13},{26,28},{27,29},{12,10},{13,11},{28,26},{29,27}} | collective-permute-start | bytes 2949128 | tf_op jit(solution)/shard_map/ppermute | solution.py:593

commit v4 on v3

--- a/solution.py
+++ b/solution.py
@@ -11,6 +11,7 @@
 RING = 2
 SLOTS = 3
 LANES = 128
+EARLY_UNITS = 3
 UNITS = 8
 GROUPS = ((0, 1), (1, 2), (3, 2), (5, 1), (6, 2))
 KEPT_UNITS = (8, 8, 4)
@@ -49,6 +50,7 @@
     half = members // 2
     side, place_in_half = me // half, lax.rem(me, half)
     unit = rows // UNITS
+    early = EARLY_UNITS * unit
 
     def peer(j):
         return lax.rem(me + j, members)
@@ -141,7 +143,7 @@
         begin, count = GROUPS[g]
         begin, count = begin * unit, count * unit
         there = pl.ds(pl.multiple_of(me * rows + begin, unit), count)
-        columns = slice(LANES, None) if far else slice(None)
+        columns = slice(LANES, None) if far and begin < early else slice(None)
         return remote(
             narrow.at[0, j, begin : begin + count, columns], final_gate.at[0, there, columns],
             group_send.at[g, j], group_recv.at[g, j], peer(j),
@@ -169,7 +171,7 @@
         )
 
     def raw_copy(piece, n):
-        count = rows // 2
+        count = early // 2
         part = slice(piece * count, (piece + 1) * count)
         return remote(
             raw.at[n, part, :], stage.at[n, part, :],
@@ -277,7 +279,7 @@
 
     @pl.loop(0, half)
     def _(n):
-        raw[n] = held[0, offset(far_peer(n)), :, 0:LANES].astype(jnp.bfloat16)
+        raw[n] = held[0, offset(far_peer(n)), 0:early, 0:LANES]
 
     @pl.loop(0, half)
     def _(n):
@@ -341,8 +343,9 @@
         for piece in range(2):
             raw_copy(piece, n).wait_recv()
         from_member = (1 - side) * half + lax.rem(place_in_half + half - n, half)
-        block = stage[n].astype(jnp.float32) * my_inverse[:, 0:LANES]
-        final_gate[0, rows_of(from_member), 0:LANES] = block.astype(jnp.bfloat16)
+        block = stage[n] * my_inverse[:, 0:LANES]
+        there = pl.ds(pl.multiple_of(from_member * rows, rows), early)
+        final_gate[0, there, 0:LANES] = block.astype(jnp.bfloat16)
 
     for n in range(1, half):
         for far in (True, False):
@@ -487,8 +490,8 @@
         scratch_shapes=[
             pltpu.VMEM((1 + RING, members, rows, inner), jnp.float32),
             pltpu.VMEM((SLOTS, members, rows, inner), jnp.bfloat16),
-            pltpu.VMEM((half, rows, LANES), jnp.bfloat16),
-            pltpu.VMEM((half, rows, LANES), jnp.bfloat16),
+            pltpu.VMEM((half, rows // UNITS * EARLY_UNITS, LANES), jnp.float32),
+            pltpu.VMEM((half, rows // UNITS * EARLY_UNITS, LANES), jnp.float32),
             sums(members), sums(members), sums(members),
             sums(members, late), sums(half, late), sums(half, late),
             sums(late), sums(late), sums(members, late),

time: 555 us -> 560 us (level)
  no operation moved by 1% of the time
where the time goes in v4:
time: 560 us
  Pallas kernels  558 us (100%)
    pallas_call x1, Pallas kernels, exchange(): pl.pallas_call(functools.partial(kernel, groups, members, local, rows), o...  550 us
  transfers between devices with their start and end apart: 1, of which 0 were waited for; matrix products, arithmetic and copies ran while one was open for 0% of the time, Pallas kernels for 2%

profile of v4, /device:TPU:12, one launch (start us, length us, event | category | flops | bytes accessed | tf_op | source)
XLA Modules:
  0.0 559.7 jit_solution(10878124710840925353)
XLA Ops:
  0.6 549.6 %shard_map.83 = (bf16[4,2048,768]{2,1,0:T(8,128)(2,1)S(1)}, bf16[4,2048,768]{2,1,0:T(8,128)(2,1)S(1)}, f32[4,768]{1,0:T(4,128)S(1)}, f32[4,768]{1,0:T(4,128)S(1)...) custom-call(f32[32,256,768]{2,1,0:T(8,128)} %gate.1, f32[32,256,768]{2,1,0:T(8,128)} %up.1, ...), custom_call_target="tpu_custom_call" | custom-call | tf_op jit(solution)/shard_map/pallas_call | solution.py:481
  550.2 0.7 collective-permute-start
  551.0 8.6 %shard_map.84 = (bf16[4,2048,768]{2,1,0:T(8,128)(2,1)}, bf16[4,2048,768]{2,1,0:T(8,128)(2,1)}, f32[4,768]{1,0:T(4,128)}, f32[4,768]{1,0:T(4,128)}, bf16[2048,128]{1,0:T(8,128)(2,1)}) custom-call(bf16[4,2048,768]{2,1,0:T(8,128)(2,1)S(1)} %get-tuple-element.16.refs_0_, bf16[4,2048,768]{2,1,0:T(8,128)(2,1)S(1)} %get-tuple-element.17.refs_1_, ...), custom_call_target="tpu_custom_call" | custom-call | flops 20000000 | bytes 1000 | tf_op jit(solution)/shard_map/pallas_call | solution.py:535
  559.6 0.0 collective-permute-done.moved
  559.6 0.1 shard_map.85
Async XLA Ops:
  550.2 9.4 %collective-permute-start = (bf16[640,768]{1,0:T(8,128)(2,1)S(1)}, bf16[640,768]{1,0:T(8,128)(2,1)S(1)}, u32[]{:S(2)}, u32[]{:S(2)}) collective-permute-start(bf16[640,768]{1,0:T(8,128)(2,1)S(1)} %get-tuple-element.22), channel_id=1, source_target_pairs={{10,12},{11,13},{26,28},{27,29},{12,10},{13,11},{28,26},{29,27}} | collective-permute-start | bytes 2949128 | tf_op jit(solution)/shard_map/ppermute | solution.py:596
